TPU v7x, 32 devices: a whole 2x2x4 slice. The times are simulated.
32 devices in a mesh: row: 8 (over y, x, core), col: 4 (over z).
Axes of the slice: x: 2, y: 2, z: 4, core: 2. Of those that a mesh axis runs over, the one named last changes fastest.
Arguments:
- density_start: float32 [512, 512], P('row', 'col'), may hold values from -0.5 to 1, as said below
- branches: int32 [6], replicated, may hold values from 0 to 1, as said below
Outputs:
- density: float32 [512, 512], P('row', 'col')
- occupations: float32 [6, 2], replicated
Inputs may be any that keep to these rules, and one draw needn't show every extreme that they name: density_start is symmetric with eigenvalues inside 0 to 1. `branches`: each entry is 0 or 1, and exactly 3 entries are 1.
All inputs are finite; a program needn't handle non-finite values.
Results may differ from a plain program's by a relative error of at most 0.0025.
Values may be sent and summed in bfloat16 or wider, within the bound.
A program may use at most 64 MiB of HBM per device.

v0:
```python
import jax
import jax.numpy as jnp
from jax import lax
from jax.sharding import PartitionSpec as P

ITERS = 6


def taken_in(shard, axis, dim, absorb, state):
    everything = jax.tree.map(lambda a: lax.all_gather(a, axis, axis=dim, tiled=True), shard)
    return absorb(state, everything, jnp.int32(0))


def local_trace(matrix_block, diagonal_mask):
    return jnp.sum(matrix_block * diagonal_mask)


def body(density_start, branches):
    rows_here, cols_here = density_start.shape
    row_first = lax.axis_index("row") * rows_here
    col_first = lax.axis_index("col") * cols_here
    row_ids = row_first + lax.broadcasted_iota(jnp.int32, (rows_here, cols_here), 0)
    col_ids = col_first + lax.broadcasted_iota(jnp.int32, (rows_here, cols_here), 1)
    diagonal_mask = (row_ids == col_ids).astype(jnp.float32)
    size_total = cols_here * lax.axis_size("col")
    density = density_start
    records = []
    for iteration in range(ITERS):
        narrow = density.astype(jnp.bfloat16)
        empty = jnp.zeros((rows_here, cols_here), jnp.float32)
        plain_local = local_trace(density, diagonal_mask)
        row_panel = lax.all_gather(narrow, "col", axis=1, tiled=True)

        def add_rows(accumulated, shard_piece, offset):
            panel_part = lax.dynamic_slice_in_dim(row_panel, offset, shard_piece.shape[0], 1)
            return accumulated + jnp.dot(
                panel_part, shard_piece, preferred_element_type=jnp.float32
            )

        square = taken_in(narrow, "row", 0, add_rows, empty)
        square_local = local_trace(square, diagonal_mask)
        branch_now = branches[iteration]
        records.append(jnp.stack([plain_local, square_local]))
        density = jnp.where(branch_now == 1, 2.0 * density - square, square)
    stacked = jnp.stack(records)
    stacked = lax.psum(stacked, ("row", "col"))
    occupations = stacked / size_total
    return (density, occupations)


def solution(mesh):
    in_specs = (P("row", "col"), P())
    out_specs = (P("row", "col"), P())
    return jax.shard_map(body, mesh=mesh, in_specs=in_specs, out_specs=out_specs, check_vma=False)
```

profile of v0, /device:TPU:0, one launch (start us, length us, event | category | flops | bytes accessed | tf_op | source)
XLA Modules:
  0.0 182.0 jit_solution(16147823306401190443)
XLA Ops:
  0.6 0.0 copy-start
  0.7 1.6 fusion.17
  6.1 0.0 copy-done
  6.1 13.7 %all_gather.36 = bf16[64,512]{1,0:T(8,128)(2,1)S(1)} all-gather(bf16[64,128]{1,0:T(8,128)(2,1)S(1)} %convert_element_type.19), channel_id=1, replica_groups=mesh['row'=8,'col'=4] {'col'}, dimensions={1}, use_global_device_ids=true | all-gather | bytes 81920 | tf_op jit(solution)/shard_map/all_gather | solution.py:32
  19.8 9.2 %all_gather.37 = bf16[512,128]{1,0:T(8,128)(2,1)S(1)} all-gather(bf16[64,128]{1,0:T(8,128)(2,1)S(1)} %convert_element_type.19), channel_id=1, replica_groups=mesh['row'=8,'col'=4] {'row'}, dimensions={0}, use_global_device_ids=true | all-gather | bytes 147456 | tf_op jit(solution)/shard_map/all_gather | solution.py:10
  29.0 0.2 fusion.16
  29.2 12.0 %all_gather.38 = bf16[64,512]{1,0:T(8,128)(2,1)S(1)} all-gather(bf16[64,128]{1,0:T(8,128)(2,1)S(1)} %get-tuple-element.24), channel_id=1, replica_groups=mesh['row'=8,'col'=4] {'col'}, dimensions={1}, use_global_device_ids=true | all-gather | bytes 81920 | tf_op jit(solution)/shard_map/all_gather | solution.py:32
  41.2 9.2 %all_gather.39 = bf16[512,128]{1,0:T(8,128)(2,1)S(1)} all-gather(bf16[64,128]{1,0:T(8,128)(2,1)S(1)} %get-tuple-element.24), channel_id=1, replica_groups=mesh['row'=8,'col'=4] {'row'}, dimensions={0}, use_global_device_ids=true | all-gather | bytes 147456 | tf_op jit(solution)/shard_map/all_gather | solution.py:10
  50.4 0.2 fusion.15
  50.5 12.0 %all_gather.40 = bf16[64,512]{1,0:T(8,128)(2,1)S(1)} all-gather(bf16[64,128]{1,0:T(8,128)(2,1)S(1)} %get-tuple-element.22), channel_id=1, replica_groups=mesh['row'=8,'col'=4] {'col'}, dimensions={1}, use_global_device_ids=true | all-gather | bytes 81920 | tf_op jit(solution)/shard_map/all_gather | solution.py:32
  62.5 8.2 %all_gather.41 = bf16[512,128]{1,0:T(8,128)(2,1)S(1)} all-gather(bf16[64,128]{1,0:T(8,128)(2,1)S(1)} %get-tuple-element.22), channel_id=1, replica_groups=mesh['row'=8,'col'=4] {'row'}, dimensions={0}, use_global_device_ids=true | all-gather | bytes 147456 | tf_op jit(solution)/shard_map/all_gather | solution.py:10
  70.7 0.2 fusion.14
  70.9 12.0 %all_gather.42 = bf16[64,512]{1,0:T(8,128)(2,1)S(1)} all-gather(bf16[64,128]{1,0:T(8,128)(2,1)S(1)} %get-tuple-element.20), channel_id=1, replica_groups=mesh['row'=8,'col'=4] {'col'}, dimensions={1}, use_global_device_ids=true | all-gather | bytes 81920 | tf_op jit(solution)/shard_map/all_gather | solution.py:32
  82.9 9.2 %all_gather.43 = bf16[512,128]{1,0:T(8,128)(2,1)S(1)} all-gather(bf16[64,128]{1,0:T(8,128)(2,1)S(1)} %get-tuple-element.20), channel_id=1, replica_groups=mesh['row'=8,'col'=4] {'row'}, dimensions={0}, use_global_device_ids=true | all-gather | bytes 147456 | tf_op jit(solution)/shard_map/all_gather | solution.py:10
  92.1 0.2 fusion.13
  92.2 12.0 %all_gather.44 = bf16[64,512]{1,0:T(8,128)(2,1)S(1)} all-gather(bf16[64,128]{1,0:T(8,128)(2,1)S(1)} %get-tuple-element.18), channel_id=1, replica_groups=mesh['row'=8,'col'=4] {'col'}, dimensions={1}, use_global_device_ids=true | all-gather | bytes 81920 | tf_op jit(solution)/shard_map/all_gather | solution.py:32
  104.2 8.2 %all_gather.45 = bf16[512,128]{1,0:T(8,128)(2,1)S(1)} all-gather(bf16[64,128]{1,0:T(8,128)(2,1)S(1)} %get-tuple-element.18), channel_id=1, replica_groups=mesh['row'=8,'col'=4] {'row'}, dimensions={0}, use_global_device_ids=true | all-gather | bytes 147456 | tf_op jit(solution)/shard_map/all_gather | solution.py:10
  112.4 0.2 fusion.12
  112.6 12.0 %all_gather.46 = bf16[64,512]{1,0:T(8,128)(2,1)S(1)} all-gather(bf16[64,128]{1,0:T(8,128)(2,1)S(1)} %get-tuple-element.16), channel_id=1, replica_groups=mesh['row'=8,'col'=4] {'col'}, dimensions={1}, use_global_device_ids=true | all-gather | bytes 81920 | tf_op jit(solution)/shard_map/all_gather | solution.py:32
  124.6 9.2 %all_gather.47 = bf16[512,128]{1,0:T(8,128)(2,1)S(1)} all-gather(bf16[64,128]{1,0:T(8,128)(2,1)S(1)} %get-tuple-element.16), channel_id=1, replica_groups=mesh['row'=8,'col'=4] {'row'}, dimensions={0}, use_global_device_ids=true | all-gather | bytes 147456 | tf_op jit(solution)/shard_map/all_gather | solution.py:10
  133.8 1.5 fusion.10
  135.2 1.3 maximum_bitcast_fusion.5
  136.5 0.1 copy.10
  136.6 1.3 maximum_bitcast_fusion.4
  138.0 0.1 copy.9
  138.1 1.3 maximum_bitcast_fusion.3
  139.4 0.1 copy.8
  139.4 1.3 maximum_bitcast_fusion.2
  140.8 0.1 copy.7
  140.9 1.3 maximum_bitcast_fusion.1
  142.2 0.1 copy.6
  142.3 1.3 maximum_bitcast_fusion
  143.6 0.1 copy.5
  143.7 0.1 stack.99
  143.8 37.7 %psum.7 = f32[6,2]{0,1:T(2,128)S(1)} all-reduce(f32[6,2]{0,1:T(2,128)S(1)} %stack.99), channel_id=1, replica_groups=mesh['row'=8,'col'=4] {'row','col'}, use_global_device_ids=true, to_apply=%region_12.13 | all-reduce | flops 12 | bytes 96 | tf_op jit(solution)/shard_map/psum | solution.py:46
  181.5 0.6 broadcast_multiply_fusion
  (3 shorter events, 0.0 us)
Async XLA Ops:
  0.6 5.5 %copy-start = (f32[64,128]{1,0:T(8,128)S(1)}, f32[64,128]{1,0:T(8,128)}, u32[]{:S(2)}) copy-start(f32[64,128]{1,0:T(8,128)} %param.2) | copy-start | bytes 98308
where the time goes:
time: 183 us; the launch traced here: 182 us
  blocking collectives  165 us (90%)
  other arithmetic  8.46 us (5%)
  between operations  4.56 us (2%)
  matrix products  2.26 us (1%)
  local copies, waits for them, and re-layouts  2.23 us (1%)
    all_gather x6, blocking collectives, body(): row_panel = lax.all_gather(narrow, 'col', axis=1, tiled=True)  73.7 us
    all_gather x6, blocking collectives, taken_in(): lax.all_gather(a, axis, axis=dim, tiled=True)  53.2 us
    psum x1, blocking collectives, body(): stacked = lax.psum(stacked, ('row', 'col'))  37.7 us
    another operation x6, other arithmetic, body(): stacked = jnp.stack(records)  7.88 us

commit v1 on v0

--- a/solution.py
+++ b/solution.py
@@ -43,7 +43,7 @@
         records.append(jnp.stack([plain_local, square_local]))
         density = jnp.where(branch_now == 1, 2.0 * density - square, square)
     stacked = jnp.stack(records)
-    stacked = lax.psum(stacked, ("row", "col"))
+    stacked = lax.psum(lax.psum(stacked, "col"), "row")
     occupations = stacked / size_total
     return (density, occupations)
 

time: 183 us -> 165 us (0.902)
  blocking collectives: 165 us -> 147 us
    psum x1 -> x2, blocking collectives: 37.7 us -> 20.1 us  [body(): stacked = lax.psum(lax.psum(stacked, 'col'), 'row')]
where the time goes in v1:
time: 165 us; the launch traced here: 164 us
  blocking collectives  147 us (89%)
  other arithmetic  8.46 us (5%)
  between operations  4.56 us (3%)
  matrix products  2.26 us (1%)
  local copies, waits for them, and re-layouts  2.23 us (1%)
    all_gather x6, blocking collectives, body(): row_panel = lax.all_gather(narrow, 'col', axis=1, tiled=True)  73.7 us
    all_gather x6, blocking collectives, taken_in(): lax.all_gather(a, axis, axis=dim, tiled=True)  53.2 us
    psum x2, blocking collectives, body(): stacked = lax.psum(lax.psum(stacked, 'col'), 'row')  20.1 us
    another operation x6, other arithmetic, body(): stacked = jnp.stack(records)  7.88 us

profile of v1, /device:TPU:0, one launch (start us, length us, event | category | flops | bytes accessed | tf_op | source)
XLA Modules:
  0.0 164.5 jit_solution(430901610562500738)
XLA Ops:
  0.6 0.0 copy-start
  0.7 1.6 fusion.17
  6.1 0.0 copy-done
  6.1 13.7 %all_gather.36 = bf16[64,512]{1,0:T(8,128)(2,1)S(1)} all-gather(bf16[64,128]{1,0:T(8,128)(2,1)S(1)} %convert_element_type.19), channel_id=1, replica_groups=mesh['row'=8,'col'=4] {'col'}, dimensions={1}, use_global_device_ids=true | all-gather | bytes 81920 | tf_op jit(solution)/shard_map/all_gather | solution.py:32
  19.8 9.2 %all_gather.37 = bf16[512,128]{1,0:T(8,128)(2,1)S(1)} all-gather(bf16[64,128]{1,0:T(8,128)(2,1)S(1)} %convert_element_type.19), channel_id=1, replica_groups=mesh['row'=8,'col'=4] {'row'}, dimensions={0}, use_global_device_ids=true | all-gather | bytes 147456 | tf_op jit(solution)/shard_map/all_gather | solution.py:10
  29.0 0.2 fusion.16
  29.2 12.0 %all_gather.38 = bf16[64,512]{1,0:T(8,128)(2,1)S(1)} all-gather(bf16[64,128]{1,0:T(8,128)(2,1)S(1)} %get-tuple-element.24), channel_id=1, replica_groups=mesh['row'=8,'col'=4] {'col'}, dimensions={1}, use_global_device_ids=true | all-gather | bytes 81920 | tf_op jit(solution)/shard_map/all_gather | solution.py:32
  41.2 9.2 %all_gather.39 = bf16[512,128]{1,0:T(8,128)(2,1)S(1)} all-gather(bf16[64,128]{1,0:T(8,128)(2,1)S(1)} %get-tuple-element.24), channel_id=1, replica_groups=mesh['row'=8,'col'=4] {'row'}, dimensions={0}, use_global_device_ids=true | all-gather | bytes 147456 | tf_op jit(solution)/shard_map/all_gather | solution.py:10
  50.4 0.2 fusion.15
  50.5 12.0 %all_gather.40 = bf16[64,512]{1,0:T(8,128)(2,1)S(1)} all-gather(bf16[64,128]{1,0:T(8,128)(2,1)S(1)} %get-tuple-element.22), channel_id=1, replica_groups=mesh['row'=8,'col'=4] {'col'}, dimensions={1}, use_global_device_ids=true | all-gather | bytes 81920 | tf_op jit(solution)/shard_map/all_gather | solution.py:32
  62.5 8.2 %all_gather.41 = bf16[512,128]{1,0:T(8,128)(2,1)S(1)} all-gather(bf16[64,128]{1,0:T(8,128)(2,1)S(1)} %get-tuple-element.22), channel_id=1, replica_groups=mesh['row'=8,'col'=4] {'row'}, dimensions={0}, use_global_device_ids=true | all-gather | bytes 147456 | tf_op jit(solution)/shard_map/all_gather | solution.py:10
  70.7 0.2 fusion.14
  70.9 12.0 %all_gather.42 = bf16[64,512]{1,0:T(8,128)(2,1)S(1)} all-gather(bf16[64,128]{1,0:T(8,128)(2,1)S(1)} %get-tuple-element.20), channel_id=1, replica_groups=mesh['row'=8,'col'=4] {'col'}, dimensions={1}, use_global_device_ids=true | all-gather | bytes 81920 | tf_op jit(solution)/shard_map/all_gather | solution.py:32
  82.9 9.2 %all_gather.43 = bf16[512,128]{1,0:T(8,128)(2,1)S(1)} all-gather(bf16[64,128]{1,0:T(8,128)(2,1)S(1)} %get-tuple-element.20), channel_id=1, replica_groups=mesh['row'=8,'col'=4] {'row'}, dimensions={0}, use_global_device_ids=true | all-gather | bytes 147456 | tf_op jit(solution)/shard_map/all_gather | solution.py:10
  92.1 0.2 fusion.13
  92.2 12.0 %all_gather.44 = bf16[64,512]{1,0:T(8,128)(2,1)S(1)} all-gather(bf16[64,128]{1,0:T(8,128)(2,1)S(1)} %get-tuple-element.18), channel_id=1, replica_groups=mesh['row'=8,'col'=4] {'col'}, dimensions={1}, use_global_device_ids=true | all-gather | bytes 81920 | tf_op jit(solution)/shard_map/all_gather | solution.py:32
  104.2 8.2 %all_gather.45 = bf16[512,128]{1,0:T(8,128)(2,1)S(1)} all-gather(bf16[64,128]{1,0:T(8,128)(2,1)S(1)} %get-tuple-element.18), channel_id=1, replica_groups=mesh['row'=8,'col'=4] {'row'}, dimensions={0}, use_global_device_ids=true | all-gather | bytes 147456 | tf_op jit(solution)/shard_map/all_gather | solution.py:10
  112.4 0.2 fusion.12
  112.6 12.0 %all_gather.46 = bf16[64,512]{1,0:T(8,128)(2,1)S(1)} all-gather(bf16[64,128]{1,0:T(8,128)(2,1)S(1)} %get-tuple-element.16), channel_id=1, replica_groups=mesh['row'=8,'col'=4] {'col'}, dimensions={1}, use_global_device_ids=true | all-gather | bytes 81920 | tf_op jit(solution)/shard_map/all_gather | solution.py:32
  124.6 9.2 %all_gather.47 = bf16[512,128]{1,0:T(8,128)(2,1)S(1)} all-gather(bf16[64,128]{1,0:T(8,128)(2,1)S(1)} %get-tuple-element.16), channel_id=1, replica_groups=mesh['row'=8,'col'=4] {'row'}, dimensions={0}, use_global_device_ids=true | all-gather | bytes 147456 | tf_op jit(solution)/shard_map/all_gather | solution.py:10
  133.8 1.5 fusion.10
  135.2 1.3 maximum_bitcast_fusion.5
  136.5 0.1 copy.10
  136.6 1.3 maximum_bitcast_fusion.4
  138.0 0.1 copy.9
  138.1 1.3 maximum_bitcast_fusion.3
  139.4 0.1 copy.8
  139.4 1.3 maximum_bitcast_fusion.2
  140.8 0.1 copy.7
  140.9 1.3 maximum_bitcast_fusion.1
  142.2 0.1 copy.6
  142.3 1.3 maximum_bitcast_fusion
  143.6 0.1 copy.5
  143.7 0.1 stack.99
  143.8 8.3 %psum.14 = f32[6,2]{0,1:T(2,128)S(1)} all-reduce(f32[6,2]{0,1:T(2,128)S(1)} %stack.99), channel_id=1, replica_groups=mesh['row'=8,'col'=4] {'col'}, use_global_device_ids=true, to_apply=%region_12.13 | all-reduce | flops 12 | bytes 96 | tf_op jit(solution)/shard_map/psum | solution.py:46
  152.1 11.8 %psum.15 = f32[6,2]{0,1:T(2,128)S(1)} all-reduce(f32[6,2]{0,1:T(2,128)S(1)} %psum.14), channel_id=1, replica_groups=mesh['row'=8,'col'=4] {'row'}, use_global_device_ids=true, to_apply=%region_13.14 | all-reduce | flops 12 | bytes 96 | tf_op jit(solution)/shard_map/psum | solution.py:46
  163.9 0.6 broadcast_multiply_fusion
  (3 shorter events, 0.0 us)
Async XLA Ops:
  0.6 5.5 %copy-start = (f32[64,128]{1,0:T(8,128)S(1)}, f32[64,128]{1,0:T(8,128)}, u32[]{:S(2)}) copy-start(f32[64,128]{1,0:T(8,128)} %param.2) | copy-start | bytes 98308
